TPU v7x, 32 devices: a whole 2x2x4 slice. The times are simulated.
32 devices in a mesh: grp: 2 (over x), space: 16 (over z, y, core).
Axes of the slice: x: 2, y: 2, z: 4, core: 2. Of those that a mesh axis runs over, the one named last changes fastest.
Arguments:
- propagator: bfloat16 [4, 3, 4, 12, 32768], P('grp', None, None, None, 'space'), parts along dimension 0, may hold values from -6 to 6
- eigvecs: bfloat16 [4, 3, 256, 32768], P('grp', None, None, 'space'), parts along dimension 0, may hold values from -6 to 6
- operator_weights: float32 [256, 2, 256], P('grp'), parts along dimension 0, may hold values from -0.375 to 0.375
- sink_time: int32 [2], P('grp'), parts along dimension 0, may hold values from 0 to 127
- term_index: int32 [48, 3], replicated, may hold values from 0 to 11
- term_sign: int32 [48], replicated, may hold values from 0 to 1
- solver_order: int32 [32768], P('space'), may hold values from 0 to 32767, as said below
Outputs:
- solver_source: bfloat16 [4, 3, 4, 12, 32768], P('grp', None, None, None, 'space'), parts along dimension 0
There are 2 independent parts, one for each index of `grp`. A program takes and returns all parts, laid end to end along the dimension named above; an argument that names none is the same for every part. Nothing has to cross between parts.
Inputs may be any that keep to these rules, and one draw needn't show every extreme that they name: solver_order is a permutation of the sites; split into blocks of 2048 positions and each block into pieces of 128, piece d of block e holds only sites d * 2048 to (d + 1) * 2048 - 1.
All inputs are finite; a program needn't handle non-finite values.
Results may differ from a plain program's by a relative error of at most 0.006.
Values may be sent and summed in bfloat16 or wider, within the bound.
A program may use at most 64 MiB of HBM per device.

v0:
```python
import math

import jax
import jax.numpy as jnp
from jax import lax
from jax.sharding import PartitionSpec as P

NVEC = 256
NMOM = 4
EXTENT = 64


MOMENTA = ((0, 0, 0), (1, 0, 0), (0, 1, 0), (0, 0, 1))
PRECISE = lax.Precision.HIGHEST


def phase_tables(offset, length):
    site_index = offset + jnp.arange(length, dtype=jnp.int32)
    coord_x = site_index % EXTENT
    coord_y = site_index // EXTENT % EXTENT
    coord_z = site_index // (EXTENT * EXTENT)
    windings = jnp.stack(
        [
            (step_x * coord_x + step_y * coord_y + step_z * coord_z) % EXTENT
            for step_x, step_y, step_z in MOMENTA
        ]
    )
    angles = windings.astype(jnp.float32) * (2.0 * math.pi / EXTENT)
    return (jnp.cos(angles), jnp.sin(angles))


def phased_rows(prop_colour, cosine_table, sine_table):
    real_part = prop_colour[0].astype(jnp.float32)[None]
    imag_part = prop_colour[1].astype(jnp.float32)[None]
    cos_rows = cosine_table[:, None, None, :]
    sin_rows = sine_table[:, None, None, :]
    turned = jnp.stack(
        [cos_rows * real_part + sin_rows * imag_part, cos_rows * imag_part - sin_rows * real_part]
    )
    return turned.astype(jnp.bfloat16).reshape(-1, turned.shape[-1])


def project(eig_colour, phased, scale_in):
    site_dims = (((1,), (1,)), ((), ()))
    from_real = lax.dot_general(
        eig_colour[0], phased, site_dims, preferred_element_type=jnp.float32
    ).reshape(-1, 2, NMOM, 48)
    from_imag = lax.dot_general(
        eig_colour[1], phased, site_dims, preferred_element_type=jnp.float32
    ).reshape(-1, 2, NMOM, 48)
    real_part = from_real[:, 0] + from_imag[:, 1]
    imag_part = from_real[:, 1] - from_imag[:, 0]
    return jnp.stack([real_part, imag_part]) * scale_in


def assemble(pieces):
    stacked = jnp.stack(pieces)
    vectors = stacked.shape[2]
    return stacked.transpose(3, 1, 2, 0, 4).reshape(NMOM, 2, vectors, 144)


def weighted_total(blocks, weights):
    real_sum = jnp.einsum("k,pkc->pc", weights[0], blocks[:, 0], precision=PRECISE) - jnp.einsum(
        "k,pkc->pc", weights[1], blocks[:, 1], precision=PRECISE
    )
    imag_sum = jnp.einsum("k,pkc->pc", weights[0], blocks[:, 1], precision=PRECISE) + jnp.einsum(
        "k,pkc->pc", weights[1], blocks[:, 0], precision=PRECISE
    )
    return jnp.stack([real_sum, imag_sum], axis=1)


def term_tables(term_index, term_sign):
    channels = jnp.arange(12, dtype=jnp.int32)
    first_pick = (term_index[:, 0:1] == channels[None]).astype(jnp.float32)
    second_pick = (term_index[:, 1:2] == channels[None]).astype(jnp.float32)
    sign_values = (2 * term_sign - 1).astype(jnp.float32)
    placement = (term_index[None, :, 2] == channels[:, None]).astype(jnp.float32) * sign_values[
        None
    ]
    return (first_pick, second_pick, placement)


def contract(blocks, weighted, first_pick, second_pick, placement):
    vectors = blocks.shape[2]
    block_grid = blocks.reshape(NMOM, 2, vectors, 12, 12)
    first_terms = jnp.einsum("mi,pqkij->pqkmj", first_pick, block_grid, precision=PRECISE)
    second_terms = jnp.einsum(
        "mi,pqij->pqmj", second_pick, weighted.reshape(NMOM, 2, 12, 12), precision=PRECISE
    )[:, :, None]
    real_part = first_terms[:, 0] * second_terms[:, 0] - first_terms[:, 1] * second_terms[:, 1]
    imag_part = first_terms[:, 0] * second_terms[:, 1] + first_terms[:, 1] * second_terms[:, 0]
    product = jnp.stack([real_part, imag_part], axis=1)
    return jnp.einsum("cm,pqkmj->pqkcj", placement, product, precision=PRECISE).reshape(
        NMOM, 2, vectors, 144
    )


def rebuild(coeffs, eig_colour, colour, cosine_table, sine_table, scale_out):
    vectors = coeffs.shape[2]
    colour_block = coeffs.reshape(NMOM, 2, vectors, 3, 48)[:, :, :, colour]
    coeff_table = colour_block.transpose(2, 1, 0, 3).reshape(vectors, 2 * NMOM * 48)
    vector_dims = (((0,), (0,)), ((), ()))
    from_real = lax.dot_general(
        coeff_table, eig_colour[0], vector_dims, preferred_element_type=jnp.float32
    ).reshape(2, NMOM, 48, -1)
    from_imag = lax.dot_general(
        coeff_table, eig_colour[1], vector_dims, preferred_element_type=jnp.float32
    ).reshape(2, NMOM, 48, -1)
    real_part = from_real[0] - from_imag[1]
    imag_part = from_real[1] + from_imag[0]
    cos_rows = cosine_table[:, None, :]
    sin_rows = sine_table[:, None, :]
    out_real = jnp.sum(cos_rows * real_part - sin_rows * imag_part, axis=0)
    out_imag = jnp.sum(cos_rows * imag_part + sin_rows * real_part, axis=0)
    return jnp.stack([out_real, out_imag]) * scale_out


def on_device(
    propagator, eigvecs, operator_weights, sink_time, term_index, term_sign, solver_order
):
    length = propagator.shape[-1]
    devices = lax.axis_size("space")
    offset = lax.axis_index("space") * length
    cosine_table, sine_table = phase_tables(offset, length)
    scale_in = 1.0 / math.sqrt(3.0 * length * devices)
    pieces = []
    for colour in range(3):
        phased = phased_rows(propagator[:, colour], cosine_table, sine_table)
        pieces.append(project(eigvecs[:, colour], phased, scale_in))
    partial_blocks = assemble(pieces)
    weights = lax.dynamic_index_in_dim(operator_weights, sink_time[0], 0, keepdims=False)
    first_pick, second_pick, placement = term_tables(term_index, term_sign)
    blocks = lax.psum(partial_blocks, "space")
    weighted = weighted_total(blocks, weights)
    coeffs = contract(blocks, weighted, first_pick, second_pick, placement).astype(jnp.bfloat16)
    scale_out = 1.0 / math.sqrt(NMOM * NVEC)
    colours = [
        rebuild(coeffs, eigvecs[:, colour], colour, cosine_table, sine_table, scale_out)
        for colour in range(3)
    ]
    source = jnp.stack(colours, axis=1).astype(jnp.bfloat16).reshape(2 * 3 * 48, length)
    wanted = lax.all_to_all(
        solver_order.reshape(devices, -1), "space", split_axis=0, concat_axis=0, tiled=True
    )
    local_index = wanted.reshape(length) - offset
    picked = jnp.take(source, local_index, axis=1)
    placed = lax.all_to_all(picked, "space", split_axis=1, concat_axis=1, tiled=True)
    return placed.reshape(2, 3, 4, 12, length)


def solution(mesh):
    return jax.shard_map(
        on_device,
        mesh=mesh,
        in_specs=(
            P("grp", None, None, None, "space"),
            P("grp", None, None, "space"),
            P("grp", None, None),
            P("grp"),
            P(),
            P(),
            P("space"),
        ),
        out_specs=P("grp", None, None, None, "space"),
        check_vma=False,
    )
```

profile of v0, /device:TPU:15, one launch (start us, length us, event | category | flops | bytes accessed | tf_op | source)
XLA Modules:
  0.0 203.2 jit_solution(521534441980782932)
XLA Ops:
  6.8 1.5 bitcast_convert_fusion.5
  10.0 2.7 %add_convert_fusion.2 = (bf16[1,4,4,12,2048]{4,3,2,1,0:T(8,128)(2,1)S(1)}, bf16[1,4,4,12,2048]{4,3,2,1,0:T(8,128)(2,1)S(1)}, bf16[1,4,4,12,2048]{4,3,2,1,0:T(8,1...) fusion(f32[4,12,2048]{2,1,0:T(8,128)S(1)} %copy.38, ...), kind=kLoop, calls=%fused_computation.16 | loop fusion | flops 9437184 | bytes 7143424 | tf_op jit(solution)/shard_map/convert.13
  13.1 1.4 convert_element_type.148
  14.4 3.2 %fusion.33 = f32[384,256]{1,0:T(8,128)} fusion(bf16[384,2048]{1,0:T(8,128)(2,1)} %convert_element_type.148, bf16[2,3,256,2048]{3,2,1,0:T(8,128)(2,1)} %param.8), kind=kOutput, calls=%fused_computation.58 | convolution fusion | flops 402653184 | bytes 3014656 | tf_op jit(solution)/shard_map/dot_general | solution.py:45
  17.6 2.7 %fusion.29 = f32[384,256]{1,0:T(8,128)} fusion(bf16[384,2048]{1,0:T(8,128)(2,1)S(1)} %copy-done.6, bf16[2,3,256,2048]{3,2,1,0:T(8,128)(2,1)} %param.8), kind=kOutput, calls=%fused_computation.54 | convolution fusion | flops 402653184 | bytes 3014656 | tf_op jit(solution)/shard_map/dot_general | solution.py:48
  20.6 1.4 convert_element_type.153
  22.0 3.2 %fusion.25 = f32[384,256]{1,0:T(8,128)} fusion(bf16[384,2048]{1,0:T(8,128)(2,1)} %convert_element_type.153, bf16[2,3,256,2048]{3,2,1,0:T(8,128)(2,1)} %param.8), kind=kOutput, calls=%fused_computation.50 | convolution fusion | flops 402653184 | bytes 3014656 | tf_op jit(solution)/shard_map/dot_general | solution.py:45
  25.2 2.7 %fusion.21 = f32[384,256]{1,0:T(8,128)} fusion(bf16[384,2048]{1,0:T(8,128)(2,1)S(1)} %copy-done.7, bf16[2,3,256,2048]{3,2,1,0:T(8,128)(2,1)} %param.8), kind=kOutput, calls=%fused_computation.46 | convolution fusion | flops 402653184 | bytes 3014656 | tf_op jit(solution)/shard_map/dot_general | solution.py:48
  28.2 1.4 convert_element_type.158
  29.5 2.4 %fusion.17 = f32[384,256]{1,0:T(8,128)S(1)} fusion(bf16[384,2048]{1,0:T(8,128)(2,1)} %convert_element_type.158, bf16[2,3,256,2048]{3,2,1,0:T(8,128)(2,1)} %param.8), kind=kOutput, calls=%fused_computation.42 | convolution fusion | flops 402653184 | bytes 3014656 | tf_op jit(solution)/shard_map/dot_general | solution.py:45
  32.0 1.9 fusion.13
  35.2 1.1 pad_maximum_fusion.3
  36.4 6.5 %all-to-all-start = ((s32[16,1,128]{2,1,0:T(1,128)}), s32[16,1,128]{2,1,0:T(1,128)S(1)}, u32[]{:S(2)}, u32[]{:S(2)}) async-start(s32[16,1,128]{2,1,0:T(1,128)} %bitcast), calls=%async_computation | async-start | bytes 16384 | tf_op jit(solution)/shard_map/all_to_all | solution.py:142
  43.6 3.1 %all-to-all-done = s32[16,1,128]{2,1,0:T(1,128)S(1)} async-done(((s32[16,1,128]{2,1,0:T(1,128)}), s32[16,1,128]{2,1,0:T(1,128)S(1)}, u32[]{:S(2)}, u32[]{:S(2)}) %all-to-all-start) | async-done | bytes 8224 | tf_op jit(solution)/shard_map/all_to_all | solution.py:142
  46.8 82.6 %all-reduce.2.cloned.1.call-done = f32[4,2,256,144]{2,3,1,0:T(8,128)} async-done(((f32[4,2,256,144]{2,3,1,0:T(8,128)}), f32[4,2,256,144]{2,3,1,0:T(8,128)}) %all-reduce.2.cloned.1.call-update) | async-done | bytes 1179664 | tf_op jit(solution)/shard_map/psum | solution.py:133
  129.4 1.7 fusion.51
  131.1 1.7 fusion.53
  134.6 0.9 copy.46
  135.5 2.1 %convolution_bitcast_fusion = f32[4,2,256,48,12]{2,3,4,1,0:T(8,128)S(1)} fusion(f32[4,2,256,12,12]{2,1,4,3,0:T(2,128)S(1)} %bitcast.204, s32[48]{0:T(128)S(1)} %get-tuple-element.55), kind=kOutput, calls=%fused_computation.7 | convolution fusion | flops 169869888 | bytes 5898432 | tf_op jit(solution)/shard_map/mi,pqkij->pqkmj/dot_general | solution.py:86
  138.5 2.5 %fusion.8 = bf16[4,2,256,12,12]{2,3,4,1,0:T(8,128)(2,1)S(1)} fusion(f32[4,1,256,48,12]{2,3,4,1,0:T(8,128)S(1)} %get-tuple-element.24, f32[4,1,256,48,12]{2,3,4,1,0:T(8,128)S(1)} %get-tuple-element.23, f32[48]{0:T(128)S(1)} %add_convert_fusion.4, s32[48]{0:T(128)S(1)} %get-tuple-element.54), kind=kOutput, calls=%fused_computation.31 | convolution fusion | flops 171345024 | bytes 5308800 | tf_op jit(solution)/shard_map/cm,pqkmj->pqkcj/dot_general | solution.py:93
  147.9 1.4 subtract_reduce_fusion.2
  150.4 7.5 %gather_fusion = bf16[2048,288]{1,0:T(8,128)(2,1)S(1)} fusion(bf16[288,2048]{0,1:T(8,128)(2,1)S(1)} %copy.57, s32[2048]{0:T(1024)S(1)} %broadcast_clamp_fusion), kind=kCustom, calls=%fused_computation | custom fusion | bytes 2367488 | tf_op jit(solution)/shard_map/jit(_take)/gather | solution.py:146
  158.9 34.1 %all_to_all.15 = bf16[288,16,128]{2,0,1:T(8,128)(2,1)S(1)} all-to-all(bf16[288,16,128]{2,0,1:T(8,128)(2,1)S(1)} %broadcast_select_fusion), channel_id=1, replica_groups=mesh['grp'=2,'space'=16] {'space'}, dimensions={1} | all-to-all | bytes 2359296 | tf_op jit(solution)/shard_map/all_to_all | solution.py:147
  194.4 1.9 copy.60
  (95 shorter events, 16.8 us)
Async XLA Ops:
  6.5 122.8 %copy-start = (f32[128,2,256]{2,1,0:T(2,128)S(1)}, f32[128,2,256]{2,1,0:T(2,128)}, u32[]{:S(2)}) copy-start(f32[128,2,256]{2,1,0:T(2,128)} %param.9) | copy-start | bytes 786436
  6.5 122.8 %all-reduce.2.cloned.1.call-start = ((), (), s32[]{:S(2)}) async-start(), calls=%async_computation.2 | async-start | bytes 2359296 | tf_op jit(solution)/shard_map/psum | solution.py:133
  14.4 3.2 %copy-start.6 = (bf16[384,2048]{1,0:T(8,128)(2,1)S(1)}, bf16[384,2048]{1,0:T(8,128)(2,1)}, u32[]{:S(2)}) copy-start(bf16[384,2048]{1,0:T(8,128)(2,1)} %convert_element_type.148) | copy-start | bytes 4718596
  17.6 2.7 %copy-start.4 = (bf16[1,4,4,12,2048]{4,3,2,1,0:T(8,128)(2,1)S(1)}, bf16[1,4,4,12,2048]{4,3,2,1,0:T(8,128)(2,1)}, u32[]{:S(2)}) copy-start(bf16[1,4,4,12,2048]{4,3,2,1,0:T(8,128)(2,1)} %get-tuple-element.48) | copy-start | bytes 2359300
  17.6 2.7 %copy-start.5 = (bf16[1,4,4,12,2048]{4,3,2,1,0:T(8,128)(2,1)S(1)}, bf16[1,4,4,12,2048]{4,3,2,1,0:T(8,128)(2,1)}, u32[]{:S(2)}) copy-start(bf16[1,4,4,12,2048]{4,3,2,1,0:T(8,128)(2,1)} %get-tuple-element.49) | copy-start | bytes 2359300
  22.0 3.2 %copy-start.7 = (bf16[384,2048]{1,0:T(8,128)(2,1)S(1)}, bf16[384,2048]{1,0:T(8,128)(2,1)}, u32[]{:S(2)}) copy-start(bf16[384,2048]{1,0:T(8,128)(2,1)} %convert_element_type.153) | copy-start | bytes 4718596
  25.2 2.7 %copy-start.3 = (bf16[1,4,4,12,2048]{4,3,2,1,0:T(8,128)(2,1)S(1)}, bf16[1,4,4,12,2048]{4,3,2,1,0:T(8,128)(2,1)}, u32[]{:S(2)}) copy-start(bf16[1,4,4,12,2048]{4,3,2,1,0:T(8,128)(2,1)} %get-tuple-element.51) | copy-start | bytes 2359300
  29.5 2.4 %copy-start.8 = (bf16[384,2048]{1,0:T(8,128)(2,1)S(1)}, bf16[384,2048]{1,0:T(8,128)(2,1)}, u32[]{:S(2)}) copy-start(bf16[384,2048]{1,0:T(8,128)(2,1)} %convert_element_type.158) | copy-start | bytes 4718596
  32.0 2.0 copy-start.11
  32.0 2.0 copy-start.12
  33.9 1.0 copy-start.9
  33.9 1.1 copy-start.10
  35.2 7.7 %copy-start.13 = (s32[48,3]{0,1:T(4,128)S(1)}, s32[48,3]{0,1:T(4,128)}, u32[]{:S(2)}) copy-start(s32[48,3]{0,1:T(4,128)} %param.11) | copy-start | bytes 1732
  35.2 7.7 %copy-start.14 = (s32[48]{0:T(128)S(1)}, s32[48]{0:T(128)}, u32[]{:S(2)}) copy-start(s32[48]{0:T(128)} %param.12) | copy-start | bytes 580
  36.4 10.3 %all-to-all-start = ((s32[16,1,128]{2,1,0:T(1,128)}), s32[16,1,128]{2,1,0:T(1,128)S(1)}, u32[]{:S(2)}, u32[]{:S(2)}) async-start(s32[16,1,128]{2,1,0:T(1,128)} %bitcast), calls=%async_computation | async-start | bytes 16384 | tf_op jit(solution)/shard_map/all_to_all | solution.py:142
  129.4 3.6 %copy-start.2 = (f32[4,2,256,144]{2,3,1,0:T(8,128)S(1)}, f32[4,2,256,144]{2,3,1,0:T(8,128)}, u32[]{:S(2)}) copy-start(f32[4,2,256,144]{2,3,1,0:T(8,128)} %all-reduce.2.cloned.1.call-done) | copy-start | bytes 3538948
  135.5 6.7 %slice-start = ((s8[6291456]{0:T(1024)(128)(4,1)}), s8[4194304]{0:T(1024)(128)(4,1)S(1)}, s32[]{:S(2)}) async-start(s8[6291456]{0:T(1024)(128)(4,1)} %bitcast.211), calls=%async_computation.3 | async-start | bytes 8388608
  137.7 4.6 %slice-start.1 = ((s8[6291456]{0:T(1024)(128)(4,1)}), s8[2097152]{0:T(1024)(128)(4,1)S(1)}, s32[]{:S(2)}) async-start(s8[6291456]{0:T(1024)(128)(4,1)} %bitcast.211), calls=%async_computation.4 | async-start | bytes 4194304
  193.6 2.8 %copy-start.1 = (f32[128,2,256]{2,1,0:T(2,128)S(1)}, f32[128,2,256]{2,1,0:T(2,128)}, u32[]{:S(2)}) copy-start(f32[128,2,256]{2,1,0:T(2,128)} %param.9) | copy-start | bytes 786436
Sparse Core Ops, SparseCore 0:
  36.5 92.8 all-reduce.1
where the time goes:
time: 206 us; the launch traced here: 203 us
  waiting for transfers between devices  85.7 us (42%)
  blocking collectives  34.1 us (17%)
  matrix products  29 us (14%)
  local copies, waits for them, and re-layouts  21.5 us (10%)
  between operations  14.6 us (7%)
  other arithmetic  11.7 us (6%)
  starting transfers between devices  6.54 us (3%)
    psum x1, waiting for transfers between devices, on_device(): blocks = lax.psum(partial_blocks, 'space')  82.6 us
    all_to_all x1, blocking collectives, on_device(): lax.all_to_all(picked, 'space', split_axis=1, concat_axis=1, tiled=True)  34.1 us
    dot_general x3, matrix products, project(): lax.dot_general(eig_colour[0], phased, site_dims, preferred_element_type=...  8.78 us
    gather x2, local copies, waits for them, and re-layouts, on_device(): picked = jnp.take(source, local_index, axis=1)  8.36 us
    dot_general x3, matrix products, project(): lax.dot_general(eig_colour[1], phased, site_dims, preferred_element_type=...  7.31 us
    all_to_all x1, starting transfers between devices, on_device(): lax.all_to_all(solver_order.reshape(devices, -1), 'space', split_axis=0,...  6.53 us
    convert_element_type x3, local copies, waits for them, and re-layouts, phased_rows(): return turned.astype(jnp.bfloat16).reshape(-1, turned.shape[-1])  4.12 us
  transfers between devices with their start and end apart: 2, of which 2 were waited for; matrix products, arithmetic and copies ran while one was open for 0% of the time, Pallas kernels for 0%

commit v1 on v0

v1 whole, which is shorter than its diff:
```python
import functools
import math

import jax
import jax.numpy as jnp
from jax import lax
from jax.experimental import pallas as pl
from jax.experimental.pallas import tpu as pltpu
from jax.sharding import PartitionSpec as P

NMOM = 4
EXTENT = 64
MOMENTA = ((0, 0, 0), (1, 0, 0), (0, 1, 0), (0, 0, 1))
HIGH = lax.Precision.HIGHEST
F32 = jnp.float32
BF16 = jnp.bfloat16
MESH = pl.DeviceIdType.MESH


def phase_tables(offset, length):
    site_index = offset + jnp.arange(length, dtype=jnp.int32)
    coord_x = site_index % EXTENT
    coord_y = site_index // EXTENT % EXTENT
    coord_z = site_index // (EXTENT * EXTENT)
    windings = jnp.stack(
        [
            (step_x * coord_x + step_y * coord_y + step_z * coord_z) % EXTENT
            for step_x, step_y, step_z in MOMENTA
        ]
    )
    angles = windings.astype(F32) * (2.0 * math.pi / EXTENT)
    return jnp.concatenate([jnp.cos(angles), jnp.sin(angles)])


def term_matrices(term_index, term_sign):
    row = jnp.arange(24, dtype=jnp.int32)
    channel = 4 * (row // 8) + row % 4
    imag = (row // 4) % 2
    terms = term_index.shape[0]

    def pick(which, part):
        hit = (term_index[:, which : which + 1] == channel[None]) & (imag[None] == part)
        return hit.astype(F32)

    picks = jnp.concatenate([pick(0, 0), pick(0, 1), pick(1, 0), pick(1, 1)])
    signs = (2 * term_sign - 1).astype(F32)
    place = (pick(2, 0).T * signs[None], pick(2, 1).T * signs[None])
    return picks, jnp.concatenate(place, axis=1), terms


def swap_halves(x):
    top, bottom = x[..., :4, :], x[..., 4:, :]
    return jnp.concatenate([-bottom, top], axis=-2)


def kernel(
    n, units, terms, columns, scale_in, scale_out, chunk,
    prop, eig_hbm, trig, weights, picks, place, order, out,
    eig, acc, blocks, from_core, summed, from_chips, coeffs, lhs, source, wanted, staged,
    eig_sem, core_send, core_recv, chip_send, chip_recv, all_send, all_recv,
    fwd_send, fwd_recv, index_send, index_recv, out_send, out_recv, own_sem,
):
    me = lax.axis_index("space")
    chips = n // 2
    core = lax.rem(me, 2)
    chip = me // 2
    partner = me + 1 - 2 * core
    length = eig.shape[-1]
    nvec = eig.shape[2]
    filled = NMOM * columns // (2 * units)

    def to(device):
        return {"space": device}

    loads = []
    for colour in range(3):
        load = pltpu.make_async_copy(eig_hbm.at[:, colour], eig.at[:, colour], eig_sem.at[colour])
        load.start()
        loads.append(load)

    barrier = pltpu.get_barrier_semaphore()

    def greet(t, carry):
        pl.semaphore_signal(barrier, inc=1, device_id=to(lax.rem(me + t, n)), device_id_type=MESH)
        return carry

    lax.fori_loop(1, n, greet, 0)

    if filled < chips:
        blocks[filled:] = jnp.zeros((chips - filled,) + blocks.shape[1:], F32)

    def index_copy(slot, device, sem_slot):
        return pltpu.make_async_remote_copy(
            src_ref=order.at[slot], dst_ref=wanted.at[me],
            send_sem=index_send.at[slot], recv_sem=index_recv.at[sem_slot],
            device_id=to(device), device_id_type=MESH,
        )

    for colour in range(3):
        loads[colour].wait()
        acc[...] = jnp.zeros_like(acc)

        def project(step, carry, colour=colour):
            sites = pl.ds(pl.multiple_of(step * chunk, chunk), chunk)
            real = prop[0, colour, :, :, sites].astype(F32)
            imag = prop[1, colour, :, :, sites].astype(F32)
            straight = jnp.concatenate([real, imag], axis=1)
            crossed = jnp.concatenate([imag, -real], axis=1)
            first, second = [straight], [crossed]
            for p in range(1, NMOM):
                cosine = trig[p : p + 1, sites][None]
                sine = trig[NMOM + p : NMOM + p + 1, sites][None]
                first.append(cosine * straight + sine * crossed)
                second.append(cosine * crossed - sine * straight)
            rows = NMOM * columns * 8
            first = jnp.concatenate(first).reshape(rows, chunk).astype(BF16)
            second = jnp.concatenate(second).reshape(rows, chunk).astype(BF16)
            dims = (((1,), (1,)), ((), ()))
            acc[...] += lax.dot_general(
                first, eig[0, colour, :, sites], dims, preferred_element_type=F32
            ) + lax.dot_general(
                second, eig[1, colour, :, sites], dims, preferred_element_type=F32
            )
            return carry

        lax.fori_loop(0, length // chunk, project, 0)
        blocks[:filled, :, :, colour] = (acc[...] * scale_in).reshape(filled, 2, units, 8, nvec)
        if colour == 0:
            pl.semaphore_wait(barrier, n - 1)

            def send_index(t, carry):
                peer = lax.rem(me + t, n)
                index_copy(peer, peer, me).start()
                return carry

            lax.fori_loop(1, n, send_index, 0)
            wanted[pl.ds(me, 1)] = order[pl.ds(me, 1)]

    core_copy = pltpu.make_async_remote_copy(
        src_ref=blocks.at[:, 1 - core], dst_ref=from_core,
        send_sem=core_send, recv_sem=core_recv, device_id=to(partner), device_id_type=MESH,
    )
    core_copy.start()
    core_copy.wait()

    def chip_copy(slot, device, sem_slot):
        return pltpu.make_async_remote_copy(
            src_ref=summed.at[slot], dst_ref=from_chips.at[chip],
            send_sem=chip_send.at[slot], recv_sem=chip_recv.at[sem_slot],
            device_id=to(device), device_id_type=MESH,
        )

    def send_sum(t, carry):
        other = lax.rem(chip + t, chips)
        summed[pl.ds(other, 1)] = (
            blocks[pl.ds(other, 1), pl.ds(core, 1)][:, 0] + from_core[pl.ds(other, 1)]
        ).astype(BF16)
        chip_copy(other, other * 2 + core, chip).start()
        return carry

    lax.fori_loop(1, chips, send_sum, 0)
    acc_rows = units * 24

    def add_sum(t, total):
        other = lax.rem(chip + t, chips)
        chip_in(other).wait_recv()
        return total + from_chips[pl.ds(other, 1)].astype(F32).reshape(acc_rows, nvec)

    def chip_in(other):
        return pltpu.make_async_remote_copy(
            src_ref=summed.at[other], dst_ref=from_chips.at[other],
            send_sem=chip_send.at[other], recv_sem=chip_recv.at[other],
            device_id=to(other * 2 + core), device_id_type=MESH,
        )

    own = (blocks[pl.ds(chip, 1), pl.ds(core, 1)][:, 0] + from_core[pl.ds(chip, 1)]).reshape(
        acc_rows, nvec
    )
    total = lax.fori_loop(1, chips, add_sum, own)

    weight_real, weight_imag = weights[0:1, :], weights[1:2, :]
    for unit in range(units):
        block = total[unit * 24 : (unit + 1) * 24]
        picked = lax.dot_general(
            picks[...], block, (((1,), (0,)), ((), ())), precision=HIGH, preferred_element_type=F32
        )
        first_real, first_imag = picked[:terms], picked[terms : 2 * terms]
        other_real, other_imag = picked[2 * terms : 3 * terms], picked[3 * terms :]
        second_real = jnp.sum(
            weight_real * other_real - weight_imag * other_imag, axis=1, keepdims=True
        )
        second_imag = jnp.sum(
            weight_real * other_imag + weight_imag * other_real, axis=1, keepdims=True
        )
        product = jnp.concatenate(
            [
                first_real * second_real - first_imag * second_imag,
                first_real * second_imag + first_imag * second_real,
            ]
        )
        made = lax.dot_general(
            place[...], product, (((1,), (0,)), ((), ())), precision=HIGH,
            preferred_element_type=F32,
        )
        coeffs[pl.ds(me, 1), unit] = made.reshape(1, 3, 8, nvec).astype(BF16)

    def gather_copy(slot, device, send_slot):
        return pltpu.make_async_remote_copy(
            src_ref=coeffs.at[slot], dst_ref=coeffs.at[slot],
            send_sem=all_send.at[send_slot], recv_sem=all_recv.at[slot // 2],
            device_id=to(device), device_id_type=MESH,
        )

    def forward_copy(slot):
        return pltpu.make_async_remote_copy(
            src_ref=coeffs.at[slot], dst_ref=coeffs.at[slot],
            send_sem=fwd_send.at[slot // 2], recv_sem=fwd_recv.at[slot // 2],
            device_id=to(partner), device_id_type=MESH,
        )

    def send_coeffs(t, carry):
        other = lax.rem(chip + t, chips)
        gather_copy(me, other * 2 + core, other).start()
        return carry

    lax.fori_loop(1, chips, send_coeffs, 0)
    forward_copy(me).start()

    def relay(t, carry):
        other = lax.rem(chip + chips - t, chips)
        slot = other * 2 + core
        gather_copy(slot, slot, other).wait_recv()
        forward_copy(slot).start()
        return carry

    lax.fori_loop(1, chips, relay, 0)

    def take_forwarded(c, carry):
        forward_copy(c * 2 + 1 - core).wait_recv()
        return carry

    lax.fori_loop(0, chips, take_forwarded, 0)

    for colour in range(3):
        table = coeffs[:, :, colour].astype(F32).reshape(n * units, 8, nvec)[: NMOM * columns]
        rows = NMOM * columns * 8
        lhs[0] = table.reshape(rows, nvec).astype(BF16)
        lhs[1] = swap_halves(table).reshape(rows, nvec).astype(BF16)

        def rebuild(step, carry, colour=colour):
            sites = pl.ds(pl.multiple_of(step * chunk, chunk), chunk)
            grid = jnp.dot(
                lhs[0], eig[0, colour, :, sites], preferred_element_type=F32
            ) + jnp.dot(lhs[1], eig[1, colour, :, sites], preferred_element_type=F32)
            grid = grid.reshape(NMOM, columns, 8, chunk)
            straight, crossed = grid[0], None
            for p in range(1, NMOM):
                straight = straight + trig[p : p + 1, sites][None] * grid[p]
                turned = trig[NMOM + p : NMOM + p + 1, sites][None] * grid[p]
                crossed = turned if crossed is None else crossed + turned
            made = (straight + swap_halves(crossed)) * scale_out
            source[colour * columns * 8 : (colour + 1) * columns * 8, sites] = made.reshape(
                columns * 8, chunk
            ).astype(BF16)
            return carry

        lax.fori_loop(0, length // chunk, rebuild, 0)

    def index_in(t, carry):
        other = lax.rem(me + t, n)
        pltpu.make_async_remote_copy(
            src_ref=order.at[other], dst_ref=wanted.at[other],
            send_sem=index_send.at[other], recv_sem=index_recv.at[other],
            device_id=to(other), device_id_type=MESH,
        ).wait_recv()
        return carry

    lax.fori_loop(1, n, index_in, 0)

    piece = order.shape[-1]

    def choose(peer):
        local = wanted[pl.ds(peer, 1)][0] - me * length
        site = lax.broadcasted_iota(jnp.int32, (length, piece), 0)
        onehot = jnp.where(site == local, 1.0, 0.0).astype(BF16)
        chosen = jnp.dot(source[...], onehot, preferred_element_type=F32).astype(BF16)
        staged[pl.ds(peer, 1)] = chosen[None]

    def out_copy(slot, device, dst, sem_slot):
        return pltpu.make_async_remote_copy(
            src_ref=staged.at[slot], dst_ref=out.at[dst],
            send_sem=out_send.at[slot], recv_sem=out_recv.at[sem_slot],
            device_id=to(device), device_id_type=MESH,
        )

    def send_piece(t, carry):
        peer = lax.rem(me + t, n)
        choose(peer)
        out_copy(peer, peer, me, me).start()
        return carry

    lax.fori_loop(1, n, send_piece, 0)
    choose(me)
    keep = pltpu.make_async_copy(staged.at[me], out.at[me], own_sem)
    keep.start()

    def close(t, carry):
        peer = lax.rem(me + t, n)
        index_copy(peer, peer, me).wait_send()
        out_copy(peer, peer, me, me).wait_send()
        return carry

    def close_chips(t, carry):
        other = lax.rem(chip + t, chips)
        chip_copy(other, other * 2 + core, chip).wait_send()
        gather_copy(me, other * 2 + core, other).wait_send()
        return carry

    def close_forward(c, carry):
        forward_copy(c * 2 + core).wait_send()
        return carry

    def take_piece(t, carry):
        peer = lax.rem(me + n - t, n)
        out_copy(peer, peer, peer, peer).wait_recv()
        return carry

    lax.fori_loop(1, chips, close_chips, 0)
    lax.fori_loop(0, chips, close_forward, 0)
    lax.fori_loop(1, n, close, 0)
    lax.fori_loop(1, n, take_piece, 0)
    keep.wait()


def on_device(
    propagator, eigvecs, operator_weights, sink_time, term_index, term_sign, solver_order
):
    columns, length = propagator.shape[3:]
    nvec = eigvecs.shape[2]
    n = lax.axis_size("space")
    chips = n // 2
    piece = length // n
    units = -(-NMOM * columns // n)
    trig = phase_tables(lax.axis_index("space") * length, length)
    weights = lax.dynamic_index_in_dim(operator_weights, sink_time[0], 0, keepdims=False)
    picks, place, terms = term_matrices(term_index, term_sign)
    rows = NMOM * columns * 8
    out_rows = 3 * columns * 8
    unit = (units, 3, 8, nvec)
    vmem = pl.BlockSpec(memory_space=pltpu.VMEM)
    hbm = pl.BlockSpec(memory_space=pl.ANY)
    dma = pltpu.SemaphoreType.DMA
    gathered = pl.pallas_call(
        functools.partial(
            kernel, n, units, terms, columns, 1.0 / math.sqrt(3.0 * length * n),
            1.0 / math.sqrt(NMOM * nvec), 512,
        ),
        out_shape=jax.ShapeDtypeStruct((n, out_rows, piece), BF16),
        in_specs=[vmem, hbm, vmem, vmem, vmem, vmem, vmem],
        out_specs=hbm,
        scratch_shapes=[
            pltpu.VMEM(eigvecs.shape, BF16),
            pltpu.VMEM((rows, nvec), F32),
            pltpu.VMEM((chips, 2) + unit, F32),
            pltpu.VMEM((chips,) + unit, F32),
            pltpu.VMEM((chips,) + unit, BF16),
            pltpu.VMEM((chips,) + unit, BF16),
            pltpu.VMEM((n,) + unit, BF16),
            pltpu.VMEM((2, rows, nvec), BF16),
            pltpu.VMEM((out_rows, length), BF16),
            pltpu.VMEM((n, 1, piece), jnp.int32),
            pltpu.VMEM((n, out_rows, piece), BF16),
            dma((3,)), dma, dma, dma((chips,)), dma((chips,)), dma((chips,)), dma((chips,)),
            dma((chips,)), dma((chips,)), dma((n,)), dma((n,)), dma((n,)), dma((n,)), dma,
        ],
        compiler_params=pltpu.CompilerParams(
            collective_id=0, has_side_effects=True, vmem_limit_bytes=60 * 2**20
        ),
    )(
        propagator.transpose(0, 1, 3, 2, 4), eigvecs, trig, weights, picks, place,
        solver_order.reshape(n, 1, piece),
    )
    placed = gathered.reshape(n, 3, columns, 2, 4, piece).transpose(3, 1, 4, 2, 0, 5)
    return placed.reshape(2, 3, 4, columns, length)


def solution(mesh):
    return jax.shard_map(
        on_device,
        mesh=mesh,
        in_specs=(
            P("grp", None, None, None, "space"),
            P("grp", None, None, "space"),
            P("grp", None, None),
            P("grp"),
            P(),
            P(),
            P("space"),
        ),
        out_specs=P("grp", None, None, None, "space"),
        check_vma=False,
    )
```

time: 206 us -> 75.3 us (0.37); the launches traced: 203 us -> 75.1 us
  waiting for transfers between devices: 85.7 us -> 0 us
  Pallas kernels: 0 us -> 66.3 us
  blocking collectives: 34.1 us -> 0 us
  matrix products: 29 us -> 0 us
  local copies, waits for them, and re-layouts: 21.5 us -> 5.33 us
  between operations: 14.6 us -> 0.75 us
  other arithmetic: 11.7 us -> 2.71 us
  starting transfers between devices: 6.54 us -> 0 us
    psum x1 -> x0, waiting for transfers between devices: 82.6 us -> none  [on_device(): blocks = lax.psum(partial_blocks, 'space')]
    pallas_call x0 -> x1, Pallas kernels: none -> 66.3 us  [on_device(): pl.pallas_call(functools.partial(kernel, n, units, terms, columns, 1.0 /...]
    all_to_all x1 -> x0, blocking collectives: 34.1 us -> none  [on_device(): lax.all_to_all(picked, 'space', split_axis=1, concat_axis=1, tiled=True)]
    dot_general x19 -> x0, matrix products: 29 us -> none  [the longest x3 8.78 us: project(): lax.dot_general(eig_colour[0], phased, site_dims, preferred_element_type=...]
    gather x2 -> x0, local copies, waits for them, and re-layouts: 8.36 us -> none  [on_device(): picked = jnp.take(source, local_index, axis=1)]
    convert_element_type x11 -> x0, local copies, waits for them, and re-layouts: 6.96 us -> none  [the longest x3 4.12 us: phased_rows(): return turned.astype(jnp.bfloat16).reshape(-1, turned.shape[-1])]
    all_to_all x1 -> x0, starting transfers between devices: 6.53 us -> none  [on_device(): lax.all_to_all(solver_order.reshape(devices, -1), 'space', split_axis=0,...]
    another operation x12 -> x0, other arithmetic: 5.11 us -> none
  transfers between devices with their start and end apart: 2 -> 0, of which waited for: 2 -> 0; matrix products, arithmetic and copies ran while one was open for 0% -> 0% of each run, Pallas kernels for 0% -> 0%
where the time goes in v1:
time: 75.3 us; the launch traced here: 75.1 us
  Pallas kernels  66.3 us (88%)
  local copies, waits for them, and re-layouts  5.33 us (7%)
  other arithmetic  2.71 us (4%)
    pallas_call x1, Pallas kernels, on_device(): pl.pallas_call(functools.partial(kernel, n, units, terms, columns, 1.0 /...  66.3 us
    transpose x1, local copies, waits for them, and re-layouts, on_device(): gathered.reshape(n, 3, columns, 2, 4, piece).transpose(3, 1, 4, 2, 0, 5)  2.03 us

profile of v1, /device:TPU:15, one launch (start us, length us, event | category | flops | bytes accessed | tf_op | source)
XLA Modules:
  0.0 75.1 jit_solution(5820406523334488306)
XLA Ops:
  0.0 0.0 copy-start
  0.7 0.7 add_convert_fusion.2
  1.4 0.0 copy-done
  1.4 0.6 dynamic-slice_bitcast_fusion.weights
  2.0 0.8 %slice_bitcast_fusion = (s32[48]{0:T(128)S(1)}, s32[48]{0:T(128)S(1)}, s32[48]{0:T(128)S(1)}) fusion(s32[48,3]{0,1:T(4,128)} %param.11), kind=kLoop, calls=%fused_computation.57 | loop fusion | bytes 1152 | tf_op jit(solution)/shard_map/eq | solution.py:42
  2.8 0.1 and_select_fusion.5
  2.8 0.1 compare_and_fusion.5
  2.9 0.1 add_convert_fusion.1
  3.0 0.2 and_select_fusion
  3.2 0.1 fusion.1
  3.2 0.7 pad_maximum_fusion.1.place
  3.9 0.3 fusion.10
  4.2 0.6 pad_maximum_fusion.trig
  4.8 0.7 copy.11.picks
  5.6 66.3 %shard_map.73 = bf16[16,288,128]{2,1,0:T(8,128)(2,1)} custom-call(bf16[2,3,12,4,2048]{4,3,2,1,0:T(4,128)(2,1)} %bitcast.22, bf16[2,3,256,2048]{3,2,1,0:T(8,128)(2,1)} %eig_hbm.1, f32[8,2048]{1,0:T(8,128)} %pad_maximum_fusion.trig, f32[2,256]{1,0:T(2,128)} %dynamic-slice_bitcast_fusion.weights, f32[192,24]{1,0:T(8,128)} %copy.11.picks, ...), custom_call_target="tpu_custom_call" | custom-call | tf_op jit(solution)/shard_map/pallas_call | solution.py:353
  71.9 2.0 %copy.12 = bf16[2,3,4,12,16,128]{5,4,2,3,1,0:T(8,128)(2,1)S(1)} copy(bf16[2,3,4,12,16,128]{5,2,0,3,1,4:T(4,128)(2,1)} %bitcast.21) | data formatting | bytes 2359296 | tf_op jit(solution)/shard_map/transpose | solution.py:383
  73.9 1.2 %reshape.298 = bf16[2,3,4,12,2048]{4,2,3,1,0:T(4,128)(2,1)} reshape(bf16[2,3,4,12,16,128]{5,4,2,3,1,0:T(8,128)(2,1)S(1)} %copy.12) | data formatting | bytes 2359296 | tf_op jit(solution)/shard_map/reshape | solution.py:384
  (3 shorter events, 0.0 us)
Async XLA Ops:
  0.0 1.4 %copy-start = (f32[128,2,256]{2,1,0:T(2,128)S(1)}, f32[128,2,256]{2,1,0:T(2,128)}, u32[]{:S(2)}) copy-start(f32[128,2,256]{2,1,0:T(2,128)} %param.9) | copy-start | bytes 786436

commit v2 on v1

v2 whole, which is shorter than its diff:
```python
import functools
import math

import jax
import jax.numpy as jnp
from jax import lax
from jax.experimental import pallas as pl
from jax.experimental.pallas import tpu as pltpu
from jax.sharding import PartitionSpec as P

NMOM = 4
EXTENT = 64
MOMENTA = ((0, 0, 0), (1, 0, 0), (0, 1, 0), (0, 0, 1))
HIGH = lax.Precision.HIGHEST
F32 = jnp.float32
BF16 = jnp.bfloat16
MESH = pl.DeviceIdType.MESH


def swap_halves(x):
    top, bottom = x[..., :4, :], x[..., 4:, :]
    return jnp.concatenate([-bottom, top], axis=-2)


def dot32(a, b):
    return jnp.dot(a, b, precision=HIGH, preferred_element_type=F32)


def kernel(
    n, units, columns, scale_in, scale_out, chunk,
    prop, eig_hbm, sink, table_weights, term_rows, term_sign, order, out,
    eig, trig, acc, blocks, from_core, summed, from_chips, coeffs, lhs, source, wanted, onehot,
    staged, eig_sem, core_send, core_recv, chip_send, chip_recv, all_send, all_recv,
    fwd_send, fwd_recv, index_send, index_recv, out_send, out_recv, own_sem,
):
    me = lax.axis_index("space")
    chips = n // 2
    core = lax.rem(me, 2)
    chip = me // 2
    partner = me + 1 - 2 * core
    length = eig.shape[-1]
    nvec = eig.shape[2]
    piece = order.shape[-1]
    filled = NMOM * columns // (2 * units)
    steps = length // chunk
    rows = NMOM * columns * 8

    def each(lower, upper, body):
        def step(i, carry):
            body(i)
            return carry

        lax.fori_loop(lower, upper, step, 0)

    def remote(src, dst, send_sem, recv_sem, device):
        return pltpu.make_async_remote_copy(
            src_ref=src, dst_ref=dst, send_sem=send_sem, recv_sem=recv_sem,
            device_id={"space": device}, device_id_type=MESH,
        )

    loads = []
    for colour in range(3):
        load = pltpu.make_async_copy(eig_hbm.at[:, colour], eig.at[:, colour], eig_sem.at[colour])
        load.start()
        loads.append(load)

    barrier = pltpu.get_barrier_semaphore()
    each(1, n, lambda t: pl.semaphore_signal(
        barrier, inc=1, device_id={"space": lax.rem(me + t, n)}, device_id_type=MESH
    ))

    site = me * length + lax.broadcasted_iota(jnp.int32, (1, length), 1)
    bits = EXTENT.bit_length() - 1
    low = EXTENT - 1
    coords = (site & low, (site >> bits) & low, site >> (2 * bits))
    for p in range(1, NMOM):
        winding = sum(step * coord for step, coord in zip(MOMENTA[p], coords) if step) & low
        angle = winding.astype(F32) * (2.0 * math.pi / EXTENT)
        trig[p : p + 1, :] = jnp.cos(angle)
        trig[NMOM + p : NMOM + p + 1, :] = jnp.sin(angle)
    terms = term_rows.shape[1]
    eye = lax.broadcasted_iota(jnp.int32, (terms, terms), 0) == lax.broadcasted_iota(
        jnp.int32, (terms, terms), 1
    )
    lane = lax.broadcasted_iota(jnp.int32, (terms, 24), 1)
    lane_channel = (4 * (lane >> 3) + (lane & 3)).astype(F32)
    lane_imag = (lane >> 2) & 1
    picks = []
    for which in range(2):
        row = term_rows[which : which + 1, :].astype(F32)
        column = jnp.sum(jnp.where(eye, row, 0.0), axis=1, keepdims=True)
        for part in range(2):
            hit = (lane_channel == column) & (lane_imag == part)
            picks.append(jnp.where(hit, 1.0, 0.0))
    picks = jnp.concatenate(picks)
    sub = lax.broadcasted_iota(jnp.int32, (24, terms), 0)
    target = 4 * (sub >> 3) + (sub & 3) == term_rows[2:3, :]
    signs = (2 * term_sign[...] - 1).astype(F32)
    place_real = jnp.where(target & (((sub >> 2) & 1) == 0), signs, 0.0)
    place_imag = jnp.where(target & (((sub >> 2) & 1) == 1), signs, 0.0)
    time_index = lax.broadcasted_iota(jnp.int32, table_weights.shape, 0)
    weights = jnp.sum(jnp.where(time_index == sink[0], table_weights[...], 0.0), axis=0)
    weight_real, weight_imag = weights[0:1, :], weights[1:2, :]

    if filled < chips:
        blocks[:, filled:] = jnp.zeros((3, chips - filled) + blocks.shape[2:], F32)

    def index_copy(peer, dst, sem_slot):
        return remote(
            order.at[peer], wanted.at[dst], index_send.at[peer], index_recv.at[sem_slot], peer
        )

    def core_copy(colour):
        return remote(
            blocks.at[colour, :, 1 - core], from_core.at[colour],
            core_send.at[colour], core_recv.at[colour], partner,
        )

    def chip_copy(colour, other, dst):
        return remote(
            summed.at[colour, other], from_chips.at[colour, dst],
            chip_send.at[colour, other], chip_recv.at[colour, dst], other * 2 + core,
        )

    def send_sums(colour):
        core_copy(colour).wait()

        def send(t):
            other = lax.rem(chip + t, chips)
            summed[colour, pl.ds(other, 1)] = (
                blocks[colour, pl.ds(other, 1), pl.ds(core, 1)][:, 0]
                + from_core[colour, pl.ds(other, 1)]
            ).astype(BF16)
            chip_copy(colour, other, chip).start()

        each(1, chips, send)

    for colour in range(3):
        loads[colour].wait()
        acc[...] = jnp.zeros_like(acc)

        def project(step, colour=colour):
            sites = pl.ds(pl.multiple_of(step * chunk, chunk), chunk)
            real = prop[0, colour, :, :, sites].astype(F32)
            imag = prop[1, colour, :, :, sites].astype(F32)
            straight = jnp.concatenate([real, imag], axis=1)
            crossed = jnp.concatenate([imag, -real], axis=1)
            first, second = [straight], [crossed]
            for p in range(1, NMOM):
                cosine = trig[p : p + 1, sites][None]
                sine = trig[NMOM + p : NMOM + p + 1, sites][None]
                first.append(cosine * straight + sine * crossed)
                second.append(cosine * crossed - sine * straight)
            first = jnp.concatenate(first).reshape(rows, chunk).astype(BF16)
            second = jnp.concatenate(second).reshape(rows, chunk).astype(BF16)
            dims = (((1,), (1,)), ((), ()))
            acc[...] += lax.dot_general(
                first, eig[0, colour, :, sites], dims, preferred_element_type=F32
            ) + lax.dot_general(
                second, eig[1, colour, :, sites], dims, preferred_element_type=F32
            )

        each(0, steps, project)
        blocks[colour, :filled] = (acc[...] * scale_in).reshape(filled, 2, units, 8, nvec)
        if colour == 0:
            pl.semaphore_wait(barrier, n - 1)
            core_copy(0).start()

            def send_index(t):
                peer = lax.rem(me + t, n)
                index_copy(peer, me, me).start()

            each(1, n, send_index)
            wanted[pl.ds(me, 1)] = order[pl.ds(me, 1)]
        else:
            core_copy(colour).start()
            send_sums(colour - 1)
    send_sums(2)

    def index_in(t):
        other = lax.rem(me + t, n)
        index_copy(other, other, other).wait_recv()

    each(1, n, index_in)

    def build(peer_chip):
        position = lax.broadcasted_iota(jnp.int32, (length, piece), 0)
        for half in range(2):
            local = wanted[pl.ds(peer_chip * 2 + half, 1)][0] - me * length
            onehot[pl.ds(peer_chip, 1), :, half * piece : (half + 1) * piece] = jnp.where(
                position == local, 1.0, 0.0
            ).astype(BF16)[None]

    each(0, chips, build)

    totals = []
    for colour in range(3):
        own = blocks[colour, pl.ds(chip, 1), pl.ds(core, 1)][:, 0]
        own = (own + from_core[colour, pl.ds(chip, 1)]).reshape(units * 8, nvec)

        def add_sum(t, total, colour=colour):
            other = lax.rem(chip + chips - t, chips)
            chip_copy(colour, other, other).wait_recv()
            part = from_chips[colour, pl.ds(other, 1)].astype(F32)
            return total + part.reshape(units * 8, nvec)

        totals.append(lax.fori_loop(1, chips, add_sum, own))

    for unit in range(units):
        block = jnp.concatenate([total[unit * 8 : (unit + 1) * 8] for total in totals])
        picked = dot32(picks, block)
        first_real, first_imag = picked[:terms], picked[terms : 2 * terms]
        other_real, other_imag = picked[2 * terms : 3 * terms], picked[3 * terms :]
        second_real = jnp.sum(
            weight_real * other_real - weight_imag * other_imag, axis=1, keepdims=True
        )
        second_imag = jnp.sum(
            weight_real * other_imag + weight_imag * other_real, axis=1, keepdims=True
        )
        made = dot32(place_real, first_real * second_real - first_imag * second_imag) + dot32(
            place_imag, first_real * second_imag + first_imag * second_real
        )
        made = made.reshape(3, 8, nvec).astype(BF16)
        for colour in range(3):
            coeffs[colour, pl.ds(me, 1), unit] = made[colour : colour + 1]

    def gather_copy(colour, slot, other, device):
        return remote(
            coeffs.at[colour, slot], coeffs.at[colour, slot],
            all_send.at[colour, other], all_recv.at[colour, slot // 2], device,
        )

    def forward_copy(colour, slot):
        return remote(
            coeffs.at[colour, slot], coeffs.at[colour, slot],
            fwd_send.at[colour, slot // 2], fwd_recv.at[colour, slot // 2], partner,
        )

    for colour in range(3):
        def send_coeffs(t, colour=colour):
            other = lax.rem(chip + t, chips)
            gather_copy(colour, me, other, other * 2 + core).start()

        each(1, chips, send_coeffs)
        forward_copy(colour, me).start()

    def relay(colour):
        def pass_on(t):
            other = lax.rem(chip + chips - t, chips)
            slot = other * 2 + core
            gather_copy(colour, slot, other, slot).wait_recv()
            forward_copy(colour, slot).start()

        each(1, chips, pass_on)

    def out_copy(colour, slot, device, dst, sem_slot):
        return remote(
            staged.at[slot, colour], out.at[dst, colour],
            out_send.at[colour, slot], out_recv.at[colour, sem_slot], device,
        )

    def keep(colour):
        return pltpu.make_async_copy(
            staged.at[me, colour], out.at[me, colour], own_sem.at[colour]
        )

    relay(0)
    for colour in range(3):
        each(0, chips, lambda c, colour=colour: forward_copy(colour, c * 2 + 1 - core).wait_recv())
        table = coeffs[colour].astype(F32).reshape(n * units, 8, nvec)[: NMOM * columns]
        lhs[0] = table.reshape(rows, nvec).astype(BF16)
        lhs[1] = swap_halves(table).reshape(rows, nvec).astype(BF16)

        def rebuild(step, colour=colour):
            sites = pl.ds(pl.multiple_of(step * chunk, chunk), chunk)
            grid = jnp.dot(
                lhs[0], eig[0, colour, :, sites], preferred_element_type=F32
            ) + jnp.dot(lhs[1], eig[1, colour, :, sites], preferred_element_type=F32)
            grid = grid.reshape(NMOM, columns, 8, chunk)
            straight, crossed = grid[0], None
            for p in range(1, NMOM):
                straight = straight + trig[p : p + 1, sites][None] * grid[p]
                turned = trig[NMOM + p : NMOM + p + 1, sites][None] * grid[p]
                crossed = turned if crossed is None else crossed + turned
            made = (straight + swap_halves(crossed)) * scale_out
            source[:, sites] = made.reshape(columns * 8, chunk).astype(BF16)

        each(0, steps, rebuild)
        if colour < 2:
            relay(colour + 1)

        def choose(peer_chip, colour=colour):
            chosen = jnp.dot(
                source[...], onehot[pl.ds(peer_chip, 1)][0], preferred_element_type=F32
            ).astype(BF16)
            for half in range(2):
                staged[pl.ds(peer_chip * 2 + half, 1), colour] = chosen[
                    :, half * piece : (half + 1) * piece
                ][None]

        def send_pieces(t, colour=colour):
            other = lax.rem(chip + t, chips)
            choose(other)
            for half in range(2):
                peer = other * 2 + half
                out_copy(colour, peer, peer, me, me).start()

        each(1, chips, send_pieces)
        choose(chip)
        out_copy(colour, partner, partner, me, me).start()
        keep(colour).start()

    def close_index(t):
        peer = lax.rem(me + t, n)
        index_copy(peer, me, me).wait_send()

    each(1, n, close_index)
    for colour in range(3):
        def close(t, colour=colour):
            peer = lax.rem(me + t, n)
            out_copy(colour, peer, peer, me, me).wait_send()

        def close_chips(t, colour=colour):
            other = lax.rem(chip + t, chips)
            chip_copy(colour, other, chip).wait_send()
            gather_copy(colour, me, other, other * 2 + core).wait_send()

        def take_piece(t, colour=colour):
            peer = lax.rem(me + n - t, n)
            out_copy(colour, peer, peer, peer, peer).wait_recv()

        each(1, chips, close_chips)
        each(0, chips, lambda c, colour=colour: forward_copy(colour, c * 2 + core).wait_send())
        each(1, n, close)
        each(1, n, take_piece)
        keep(colour).wait()


def on_device(
    propagator, eigvecs, operator_weights, sink_time, term_index, term_sign, solver_order
):
    columns, length = propagator.shape[3:]
    nvec = eigvecs.shape[2]
    n = lax.axis_size("space")
    chips = n // 2
    piece = length // n
    units = -(-NMOM * columns // n)
    rows = NMOM * columns * 8
    site_rows = columns * 8
    unit = (units, 8, nvec)
    vmem = pl.BlockSpec(memory_space=pltpu.VMEM)
    smem = pl.BlockSpec(memory_space=pltpu.SMEM)
    hbm = pl.BlockSpec(memory_space=pl.ANY)
    dma = pltpu.SemaphoreType.DMA
    gathered = pl.pallas_call(
        functools.partial(
            kernel, n, units, columns, 1.0 / math.sqrt(3.0 * length * n),
            1.0 / math.sqrt(NMOM * nvec), 512,
        ),
        out_shape=jax.ShapeDtypeStruct((n, 3, site_rows, piece), BF16),
        in_specs=[vmem, hbm, smem, vmem, vmem, vmem, vmem],
        out_specs=hbm,
        scratch_shapes=[
            pltpu.VMEM(eigvecs.shape, BF16),
            pltpu.VMEM((2 * NMOM, length), F32),
            pltpu.VMEM((rows, nvec), F32),
            pltpu.VMEM((3, chips, 2) + unit, F32),
            pltpu.VMEM((3, chips) + unit, F32),
            pltpu.VMEM((3, chips) + unit, BF16),
            pltpu.VMEM((3, chips) + unit, BF16),
            pltpu.VMEM((3, n) + unit, BF16),
            pltpu.VMEM((2, rows, nvec), BF16),
            pltpu.VMEM((site_rows, length), BF16),
            pltpu.VMEM((n, 1, piece), jnp.int32),
            pltpu.VMEM((chips, length, 2 * piece), BF16),
            pltpu.VMEM((n, 3, site_rows, piece), BF16),
            dma((3,)), dma((3,)), dma((3,)), dma((3, chips)), dma((3, chips)), dma((3, chips)),
            dma((3, chips)), dma((3, chips)), dma((3, chips)), dma((n,)), dma((n,)),
            dma((3, n)), dma((3, n)), dma((3,)),
        ],
        compiler_params=pltpu.CompilerParams(
            collective_id=0, has_side_effects=True, vmem_limit_bytes=60 * 2**20
        ),
    )(
        propagator.transpose(0, 1, 3, 2, 4), eigvecs, sink_time, operator_weights,
        term_index.T, term_sign.reshape(1, -1), solver_order.reshape(n, 1, piece),
    )
    placed = gathered.reshape(n, 3, columns, 2, 4, piece).transpose(3, 1, 4, 2, 0, 5)
    return placed.reshape(2, 3, 4, columns, length)


def solution(mesh):
    return jax.shard_map(
        on_device,
        mesh=mesh,
        in_specs=(
            P("grp", None, None, None, "space"),
            P("grp", None, None, "space"),
            P("grp", None, None),
            P("grp"),
            P(),
            P(),
            P("space"),
        ),
        out_specs=P("grp", None, None, None, "space"),
        check_vma=False,
    )
```

time: 75.3 us -> 60.6 us (0.80)
  Pallas kernels: 66.3 us -> 56.6 us
  other arithmetic: 2.71 us -> 0 us
  local copies, waits for them, and re-layouts: 5.33 us -> 3.2 us
    pallas_call x1, Pallas kernels: 66.3 us -> 56.6 us  [on_device(): pl.pallas_call(functools.partial(kernel, n, units, columns, 1.0 / math.sq...]
    concatenate x3 -> x0, other arithmetic: 1.39 us -> none  [the longest x1 0.68 us: term_matrices(): return (picks, jnp.concatenate(place, axis=1), terms)]
    eq x1 -> x0, local copies, waits for them, and re-layouts: 0.8 us -> none  [pick(): term_index[:, which:which + 1] == channel[None]]
where the time goes in v2:
time: 60.6 us; the launch traced here: 60.5 us
  Pallas kernels  56.6 us (93%)
  local copies, waits for them, and re-layouts  3.2 us (5%)
  between operations  0.66 us (1%)
    pallas_call x1, Pallas kernels, on_device(): pl.pallas_call(functools.partial(kernel, n, units, columns, 1.0 / math.sq...  56.6 us
    transpose x1, local copies, waits for them, and re-layouts, on_device(): gathered.reshape(n, 3, columns, 2, 4, piece).transpose(3, 1, 4, 2, 0, 5)  2.03 us

profile of v2, /device:TPU:15, one launch (start us, length us, event | category | flops | bytes accessed | tf_op | source)
XLA Modules:
  0.0 60.5 jit_solution(12444569567358190668)
XLA Ops:
  0.7 56.6 %shard_map.73 = bf16[16,3,96,128]{3,2,1,0:T(8,128)(2,1)} custom-call(bf16[2,3,12,4,2048]{4,3,2,1,0:T(4,128)(2,1)} %bitcast.12, bf16[2,3,256,2048]{3,2,1,0:T(8,128)(2,1)} %eig_hbm.1, s32[1]{0:T(128)S(6)} %copy.9.sink, f32[128,2,256]{2,1,0:T(2,128)} %table_weights.1, s32[3,48]{1,0:T(4,128)} %bitcast.14, s32[1,48]{1,0:T(1,128)} %bitcast.15, s32[16,1,128]{2,1,0:T(1,128)} %bitcast.13), custom_call_target="tpu_custom_call" | custom-call | tf_op jit(solution)/shard_map/pallas_call | solution.py:355
  57.3 2.0 %copy.8 = bf16[2,3,4,12,16,128]{5,4,2,3,1,0:T(8,128)(2,1)S(1)} copy(bf16[2,3,4,12,16,128]{5,2,0,3,1,4:T(4,128)(2,1)} %bitcast.11) | data formatting | bytes 2359296 | tf_op jit(solution)/shard_map/transpose | solution.py:388
  59.3 1.2 %reshape.15 = bf16[2,3,4,12,2048]{4,2,3,1,0:T(4,128)(2,1)} reshape(bf16[2,3,4,12,16,128]{5,4,2,3,1,0:T(8,128)(2,1)S(1)} %copy.8) | data formatting | bytes 2359296 | tf_op jit(solution)/shard_map/reshape | solution.py:389
